TPU v7x, 32 devices: a whole 2x2x4 slice. The times are simulated.
32 devices in a mesh: prow: 8 (over z, x), pcol: 4 (over y, core).
Axes of the slice: x: 2, y: 2, z: 4, core: 2. Of those that a mesh axis runs over, the one named last changes fastest.
Arguments:
- cross_cov: float32 [4, 8, 256, 8, 4, 256], P(None, 'prow', None, None, 'pcol'), may hold values from -6 to 6
- left_factor: float32 [4, 8, 256, 512], P(None, 'prow', None, 'pcol'), may hold values from -1 to 3, as said below
- right_factor: float32 [8, 4, 256, 512], P(None, 'pcol', None, 'prow'), may hold values from -1 to 3, as said below
Outputs:
- whitened: float32 [4, 8, 256, 8, 4, 256], P(None, 'prow', None, None, 'pcol')
Inputs may be any that keep to these rules, and one draw needn't show every extreme that they name: `left_factor`: the diagonal entries of the diagonal blocks lie between 1.5 and 2. `right_factor`: the diagonal entries of the diagonal blocks lie between 1.5 and 2.
All inputs are finite; a program needn't handle non-finite values.
Results may differ from a plain program's by a relative error of at most 0.0001.
Values sent between devices are 32-bit elements; how exact they have to be, the bound alone decides.
A program may use at most 128 MiB of HBM per device.

v0:
```python
import jax
import jax.numpy as jnp
from jax import lax
from jax.sharding import PartitionSpec as P

STEPS = 2


def spread(x, axis, root):
    mine = lax.axis_index(axis) == root
    return lax.psum(jnp.where(mine, x, jnp.zeros_like(x)), axis)


def solve_left(operands):
    diag_block, owned_rows = operands
    return jax.scipy.linalg.solve_triangular(diag_block, owned_rows, lower=True)


def solve_right(operands):
    diag_block, owned_cols = operands
    return jax.scipy.linalg.solve_triangular(diag_block, owned_cols.T, lower=True).T


def nothing_left(operands):
    return jnp.zeros_like(operands[1])


def shards(cross_cov, left_factor, right_factor):
    rows_axis = lax.axis_size("prow")
    cols_axis = lax.axis_size("pcol")
    my_row = lax.axis_index("prow")
    my_col = lax.axis_index("pcol")
    row_blocks = cross_cov.shape[0]
    block_size = cross_cov.shape[2]
    col_blocks = cross_cov.shape[3]
    left_rows = lax.all_gather(left_factor, "pcol", axis=3, tiled=True)[:, 0]
    right_rows = lax.all_gather(right_factor, "prow", axis=3, tiled=True)[:, 0]
    matrix = cross_cov.reshape(row_blocks, block_size, col_blocks * block_size)
    row_index = (jnp.arange(row_blocks) * rows_axis + my_row).reshape(row_blocks, 1, 1)

    def left_update(current, solved, block_step):
        first_col = block_step * block_size
        factor = left_rows[:, :, first_col : first_col + block_size]
        update = jnp.einsum("cij,jn->cin", factor, solved, precision=lax.Precision.HIGHEST)
        return jnp.where(
            row_index > block_step,
            current - update,
            jnp.where(row_index == block_step, solved[None], current),
        )

    for block_step in range(STEPS):
        local_block = block_step // rows_axis
        first_col = block_step * block_size
        diag_block = left_rows[local_block, :, first_col : first_col + block_size]
        solved = lax.cond(
            my_row == block_step % rows_axis,
            solve_left,
            nothing_left,
            (diag_block, matrix[local_block]),
        )
        solved = spread(solved, "prow", block_step % rows_axis)
        matrix = left_update(matrix, solved, block_step)
    columns = matrix.reshape(row_blocks * block_size, col_blocks, block_size)
    col_index = (jnp.arange(col_blocks) * cols_axis + my_col).reshape(1, col_blocks, 1)

    def right_update(current, solved, block_step):
        first_col = block_step * block_size
        factor = right_rows[:, :, first_col : first_col + block_size]
        update = jnp.einsum("rj,dsj->rds", solved, factor, precision=lax.Precision.HIGHEST)
        return jnp.where(
            col_index > block_step,
            current - update,
            jnp.where(col_index == block_step, solved[:, None, :], current),
        )

    for block_step in range(STEPS):
        local_block = block_step // cols_axis
        first_col = block_step * block_size
        diag_block = right_rows[local_block, :, first_col : first_col + block_size]
        solved = lax.cond(
            my_col == block_step % cols_axis,
            solve_right,
            nothing_left,
            (diag_block, columns[:, local_block]),
        )
        solved = spread(solved, "pcol", block_step % cols_axis)
        columns = right_update(columns, solved, block_step)
    return columns.reshape(cross_cov.shape)


def solution(mesh):
    placed = (
        P(None, "prow", None, None, "pcol", None),
        P(None, "prow", None, "pcol"),
        P(None, "pcol", None, "prow"),
    )
    return jax.shard_map(
        shards,
        mesh=mesh,
        in_specs=placed,
        out_specs=P(None, "prow", None, None, "pcol", None),
        check_vma=False,
    )
```

profile of v0, /device:TPU:0, one launch (start us, length us, event | category | flops | bytes accessed | tf_op | source)
XLA Modules:
  0.0 603.9 jit_solution(9120524464685021274)
XLA Ops:
  7.3 27.1 %all-gather.3.cloned.1.call-done = f32[4,1,256,512]{3,2,0,1:T(8,128)} async-done(((f32[4,1,256,128]{3,2,0,1:T(8,128)}), f32[4,1,256,512]{3,2,0,1:T(8,128)}) %all-gather.3.cloned.1.call-update) | async-done | bytes 2097168 | tf_op jit(solution)/shard_map/all_gather | solution.py:36
  34.5 34.7 %conditional.4 = (f32[256,2048]{0,1:T(8,128)}) conditional(s32[]{:T(128)} %convert_element_type.12, () %tuple.31, (f32[4,256,512]{2,1,0:T(8,128)}, f32[4,1,256,8,1,256]{5,4,3,2,1,0:T(1,128)}) %tuple.153), branch_computations={%region_0.0_spmd, %region_1.0_spmd} | conditional | flops 1208877056 | bytes 41746636 | solution.py:55
  34.5 3.9 copy.30
  40.5 3.9 while.8
  44.4 19.7 %custom-call.8 = f32[2,128,128]{1,2,0:T(8,128)S(1)} custom-call(f32[2,128,128]{2,1,0:T(8,128)S(1)} %get-tuple-element.87), custom_call_target="InvertDiagBlocksLowerTriangular" | custom-call | tf_op jit(solution)/shard_map/cond/branch_1_fun/jit(_solve_triangular)/triangular_solve | solution.py:16
  69.2 3.1 broadcast_select_fusion.1
  72.8 20.6 %copy.28 = f32[4,1,256,8,1,256]{2,5,3,0,4,1:T(8,128)} copy(f32[4,1,256,8,1,256]{5,4,3,2,1,0:T(1,128)} %param.15) | data formatting | bytes 16777216 | tf_op args[0]
  93.5 77.4 %all-reduce.5.cloned.1.call-done = f32[256,2048]{0,1:T(8,128)} async-done(((f32[256,2048]{0,1:T(8,128)}), f32[256,2048]{0,1:T(8,128)}) %all-reduce.5.cloned.1.call-update) | async-done | bytes 2097168 | tf_op jit(solution)/shard_map/psum | solution.py:11
  170.8 13.9 %fusion.17 = f32[4,256,2048]{1,2,0:T(8,128)} fusion(f32[4,256,2048]{1,2,0:T(8,128)} %bitcast.129, f32[256,2048]{0,1:T(8,128)} %all-reduce.5.cloned.1.call-done, pred[4]{0:T(512)(128)(4,1)S(1)} %get-tuple-element.153, pred[4]{0:T(512)(128)(4,1)S(1)} %get-tuple-element.154, f32[4,256,512]{2,1,0:T(8,128)} %bitcast.139), kind=kOutput, calls=%fused_computation.58 | convolution fusion | flops 6448742400 | bytes 22020104 | tf_op jit(solution)/shard_map/cij,jn->cin/dot_general | solution.py:44
  189.1 139.6 %all-reduce.7.cloned.1.call-done = f32[256,2048]{0,1:T(8,128)} async-done(((f32[256,2048]{0,1:T(8,128)}), f32[256,2048]{0,1:T(8,128)}) %all-reduce.7.cloned.1.call-update) | async-done | bytes 2097168 | tf_op jit(solution)/shard_map/psum | solution.py:11
  328.7 14.2 %fusion.16 = f32[4,256,2048]{1,2,0:T(8,128)} fusion(f32[4,256,2048]{1,2,0:T(8,128)} %fusion.17, f32[256,2048]{0,1:T(8,128)} %all-reduce.7.cloned.1.call-done, pred[4]{0:T(512)(128)(4,1)S(1)} %get-tuple-element.155, pred[4]{0:T(512)(128)(4,1)S(1)} %get-tuple-element.156, f32[4,256,512]{2,1,0:T(8,128)S(1)} %bitcast.141), kind=kOutput, calls=%fused_computation.56 | convolution fusion | flops 6448742400 | bytes 22021120 | tf_op jit(solution)/shard_map/cij,jn->cin/dot_general | solution.py:44
  342.9 8.8 %copy.34 = f32[4,256,2048]{2,1,0:T(8,128)} copy(f32[4,256,2048]{1,2,0:T(8,128)} %fusion.16) | data formatting | bytes 16777216 | tf_op jit(solution)/shard_map/jit(_where)/select_n | solution.py:45
  351.7 10.9 %copy.53 = f32[128,8,8,256]{3,2,1,0:T(8,128)} copy(f32[128,8,8,256]{3,1,2,0:T(8,128)} %bitcast.130) | data formatting | bytes 16777216
  362.6 40.2 %all-gather.5.cloned.1.call-done = f32[8,1,256,512]{2,0,1,3:T(8,128)} async-done(((f32[8,1,256,64]{2,0,1,3:T(8,128)}), f32[8,1,256,512]{2,0,1,3:T(8,128)}) %all-gather.5.cloned.1.call-update) | async-done | bytes 4194320 | tf_op jit(solution)/shard_map/all_gather | solution.py:37
  402.8 5.3 copy.36
  408.1 36.8 %conditional.6 = (f32[1024,256]{1,0:T(8,128)S(1)}) conditional(s32[]{:T(128)} %convert_element_type.14, () %tuple.35, (f32[8,256,512]{2,1,0:T(8,128)}, f32[1024,8,256]{2,1,0:T(8,128)}) %tuple.151), branch_computations={%region_6.8_spmd, %region_7.10_spmd} | conditional | flops 604504064 | bytes 27590860 | solution.py:80
  408.3 8.7 %copy.37 = f32[1024,8,256]{0,2,1:T(8,128)} copy(f32[1024,8,256]{2,1,0:T(8,128)} %get-tuple-element.106) | data formatting | bytes 16777216 | tf_op jit(solution)/shard_map
  419.4 3.6 while.10
  423.0 19.7 %custom-call.10 = f32[2,128,128]{1,2,0:T(8,128)S(1)} custom-call(f32[2,128,128]{2,1,0:T(8,128)S(1)} %get-tuple-element.89), custom_call_target="InvertDiagBlocksLowerTriangular" | custom-call | tf_op jit(solution)/shard_map/cond/branch_1_fun/jit(_solve_triangular)/triangular_solve | solution.py:21
  446.1 34.0 %all-reduce.9.cloned.1.call-done = f32[1024,256]{1,0:T(8,128)} async-done(((f32[1024,256]{1,0:T(8,128)}), f32[1024,256]{1,0:T(8,128)}) %all-reduce.9.cloned.1.call-update) | async-done | bytes 1048592 | tf_op jit(solution)/shard_map/psum | solution.py:11
  480.2 17.0 %select_select_fusion.1 = f32[1024,8,256]{2,0,1:T(8,128)} fusion(f32[1024,8,256]{2,1,0:T(8,128)} %bitcast.127, f32[1024,256]{1,0:T(8,128)} %all-reduce.9.cloned.1.call-done, pred[8]{0:T(512)(128)(4,1)S(1)} %get-tuple-element.157, pred[8]{0:T(512)(128)(4,1)S(1)} %get-tuple-element.158, f32[8,256,512]{2,1,0:T(8,128)} %bitcast.132), kind=kOutput, calls=%fused_computation.60 | convolution fusion | flops 6448742400 | bytes 20971536 | tf_op jit(solution)/shard_map/rj,dsj->rds/dot_general | solution.py:69
  498.6 72.5 %all-reduce.11.cloned.1.call-done = f32[1024,256]{1,0:T(8,128)} async-done(((f32[1024,256]{1,0:T(8,128)}), f32[1024,256]{1,0:T(8,128)}) %all-reduce.11.cloned.1.call-update) | async-done | bytes 1048592 | tf_op jit(solution)/shard_map/psum | solution.py:11
  571.1 12.9 %select_select_fusion = f32[1024,8,256]{2,0,1:T(8,128)S(1)} fusion(f32[1024,8,256]{2,0,1:T(8,128)} %select_select_fusion.1, f32[1024,256]{1,0:T(8,128)} %all-reduce.11.cloned.1.call-done, pred[8]{0:T(512)(128)(4,1)S(1)} %get-tuple-element.159, pred[8]{0:T(512)(128)(4,1)S(1)} %get-tuple-element.160, f32[8,256,512]{2,1,0:T(8,128)} %bitcast.134), kind=kOutput, calls=%fused_computation.59 | convolution fusion | flops 6448742400 | bytes 20971536 | tf_op jit(solution)/shard_map/rj,dsj->rds/dot_general | solution.py:69
  584.0 12.7 %copy.43 = f32[4,1,256,8,1,256]{5,4,3,2,1,0:T(1,128)} copy(f32[4,1,256,8,1,256]{5,2,0,3,4,1:T(8,128)S(1)} %bitcast.128) | data formatting | bytes 16777216 | tf_op jit(solution)/shard_map/reshape | solution.py:88
  (61 shorter events, 28.9 us)
Async XLA Ops:
  6.5 27.9 %all-gather.3.cloned.1.call-start = ((), (), s32[]{:S(2)}) async-start(), calls=%async_computation | async-start | bytes 2621440 | tf_op jit(solution)/shard_map/all_gather | solution.py:36
  7.3 163.6 %all-reduce.5.cloned.1.call-start = ((), (), s32[]{:S(2)}) async-start(), calls=%async_computation.1 | async-start | bytes 4194304 | tf_op jit(solution)/shard_map/psum | solution.py:11
  72.3 256.4 %all-reduce.7.cloned.1.call-start = ((), (), s32[]{:S(2)}) async-start(), calls=%async_computation.2 | async-start | bytes 4194304 | tf_op jit(solution)/shard_map/psum | solution.py:11
  186.2 1.6 copy-start.1
  187.7 141.1 %copy-start = (f32[4,1,256,512]{3,2,0,1:T(8,128)S(1)}, f32[4,1,256,512]{3,2,0,1:T(8,128)}, u32[]{:S(2)}) copy-start(f32[4,1,256,512]{3,2,0,1:T(8,128)} %all-gather.3.cloned.1.call-done) | copy-start | bytes 6291460
  187.7 215.1 %all-gather.5.cloned.1.call-start = ((), (), s32[]{:S(2)}) async-start(), calls=%async_computation.3 | async-start | bytes 4718592 | tf_op jit(solution)/shard_map/all_gather | solution.py:37
  188.9 291.3 %all-reduce.9.cloned.1.call-start = ((), (), s32[]{:S(2)}) async-start(), calls=%async_computation.4 | async-start | bytes 2097152 | tf_op jit(solution)/shard_map/psum | solution.py:11
  446.1 125.0 %all-reduce.11.cloned.1.call-start = ((), (), s32[]{:S(2)}) async-start(), calls=%async_computation.5 | async-start | bytes 2097152 | tf_op jit(solution)/shard_map/psum | solution.py:11
Sparse Core Ops, SparseCore 0:
  8.9 25.5 all-gather.2
  72.4 98.3 all-reduce.4
  187.8 140.8 all-reduce.6
  330.7 72.0 all-gather.4
  446.2 33.9 all-reduce.8
  498.7 72.3 all-reduce.10
where the time goes:
time: 611 us; the launch traced here: 604 us
  waiting for transfers between devices  392 us (64%)
  local copies, waits for them, and re-layouts  85.6 us (14%)
  matrix products  62.9 us (10%)
  other arithmetic  48.3 us (8%)
  between operations  14 us (2%)
    psum x4, waiting for transfers between devices, spread(): return lax.psum(jnp.where(mine, x, jnp.zeros_like(x)), axis)  323 us
    all_gather x1, waiting for transfers between devices, shards(): right_rows = lax.all_gather(right_factor, 'prow', axis=3, tiled=True)[:, 0]  40.2 us
    unnamed x7, local copies, waits for them, and re-layouts  32.7 us
    dot_general x2, matrix products, right_update(): jnp.einsum('rj,dsj->rds', solved, factor, precision=lax.Precision.HIGHEST)  29.9 us
    dot_general x2, matrix products, left_update(): jnp.einsum('cij,jn->cin', factor, solved, precision=lax.Precision.HIGHEST)  28.1 us
    all_gather x1, waiting for transfers between devices, shards(): left_rows = lax.all_gather(left_factor, 'pcol', axis=3, tiled=True)[:, 0]  27.1 us
    another operation x5, other arithmetic, solve_left(): return jax.scipy.linalg.solve_triangular(diag_block, owned_rows, lower=True)  20.8 us
    another operation x4, other arithmetic, solve_right(): jax.scipy.linalg.solve_triangular(diag_block, owned_cols.T, lower=True)  20.6 us
  transfers between devices with their start and end apart: 6, of which 6 were waited for; matrix products, arithmetic and copies ran while one was open for 9% of the time, Pallas kernels for 0%

commit v1 on v0

v1 whole, which is shorter than its diff:
```python
import functools

import jax
import jax.numpy as jnp
from jax import lax
from jax.experimental import pallas as pl
from jax.experimental.pallas import tpu as pltpu
from jax.sharding import PartitionSpec as P

STEPS = 2
CORES = 2
MESH = pl.DeviceIdType.MESH
HIGHEST = lax.Precision.HIGHEST
HIGH = lax.Precision.HIGH


def comm_kernel(nx, nprow, npcol, counts, st, lx, sl, ry, top, lyg, lxg, slg, stl, rtop, ltop, send_sem, recv_sem, local_sem):
    nz = nprow // nx
    ny = npcol // CORES
    cols = st.shape[0]
    prow = lax.axis_index("prow")
    pcol = lax.axis_index("pcol")
    z, x = lax.div(prow, nx), lax.rem(prow, nx)
    y, core = lax.div(pcol, CORES), lax.rem(pcol, CORES)
    x_others = [lax.rem(x + i, nx) for i in range(1, nx)]
    y_others = [lax.rem(y + i, ny) for i in range(1, ny)]
    sibling = {"pcol": y * CORES + (CORES - 1 - core)}
    up, down = {"prow": prow + nx}, {"prow": prow - nx}
    has_up, has_down = z < nz - 1, z > 0
    x_devices = [{"prow": z * nx + other} for other in x_others]
    y_devices = [{"pcol": other * CORES + core} for other in y_others]
    always = None

    def when(cond, action):
        if cond is None:
            action()
        else:
            pl.when(cond)(action)

    def both(first, second):
        if first is None:
            return second
        if second is None:
            return first
        return jnp.logical_and(first, second)

    barrier = pltpu.get_barrier_semaphore()
    for device, cond in [(up, has_up), (down, has_down)] + [(d, always) for d in x_devices + y_devices + [sibling]]:
        when(cond, lambda device=device: pl.semaphore_signal(barrier, inc=1, device_id=device, device_id_type=MESH))
    pl.semaphore_wait(barrier, nx - 1 + ny - 1 + 1 + has_up.astype(jnp.int32) + has_down.astype(jnp.int32))

    half = [(0, 1), (1, cols - 1)]
    pieces = len(half)
    base = [0]

    def region(count):
        first = base[0]
        base[0] += count
        return first

    ly_base, b_base, lt_base = region(nprow * pieces), region(STEPS * cols), region(STEPS)
    lx_base, ltg_base = region(npcol), region(npcol)
    sl_base, stl_base, rt_base = region(STEPS), region(STEPS), region(STEPS)
    counts["recv"] = base[0]

    def ly(p, j):
        return lyg.at[p, pl.ds(half[j][0], half[j][1])], ly_base + p * pieces + j

    def b(k, j):
        return top.at[k, j], b_base + k * cols + j

    def lt(k):
        return ltop.at[pcol, k], lt_base + k

    sends = []

    def send(item, devices, source=None):
        ref, rid = item
        for device, cond in devices:
            copy = pltpu.make_async_remote_copy(
                src_ref=ref if source is None else source,
                dst_ref=ref,
                send_sem=send_sem.at[len(sends)],
                recv_sem=recv_sem.at[rid],
                device_id=device,
                device_id_type=MESH,
            )
            sends.append((copy, cond))
            when(cond, copy.start)

    def receive(item, cond):
        ref, rid = item
        copy = pltpu.make_async_remote_copy(
            src_ref=ref, dst_ref=ref, send_sem=send_sem.at[0], recv_sem=recv_sem.at[rid], device_id=sibling, device_id_type=MESH
        )
        when(cond, copy.wait_recv)

    def to(devices, cond):
        return [(d, cond) for d in devices]

    lead = both(z == 0, x < STEPS if nx > STEPS else None)
    carries = both(z > 0, x < STEPS if nx > STEPS else None)
    owner_col = pcol < STEPS

    send(lt(x), [(up, lead)] + to(x_devices, lead), lx.at[0])
    send(b(x, 0), [(up, lead)] + to(x_devices, lead), st.at[0])
    for j in range(pieces):
        part = ry.at[pl.ds(half[j][0], half[j][1])]
        send(ly(prow, j), [(up, has_up), (down, has_down)] + to(x_devices, always), part)
        if j == 0:
            send((lxg.at[pcol], lx_base + pcol), to(y_devices + [sibling], always), lx)
            send((slg.at[pcol], sl_base + pcol), to(y_devices + [sibling], owner_col), sl)
    for j in range(1, cols):
        send(b(x, j), [(up, lead)] + to(x_devices, lead), st.at[j])
    locals_ = []

    def keep(source, ref, cond):
        copy = pltpu.make_async_copy(source, ref, local_sem.at[len(locals_)])
        locals_.append((copy, cond))
        when(cond, copy.start)

    keep(ry, lyg.at[prow], always)
    keep(lx, lxg.at[pcol], always)
    keep(sl, slg.at[pcol], owner_col)
    keep(st, top.at[prow], prow < STEPS)
    keep(lx.at[0], ltop.at[pcol, prow], prow < STEPS)

    def relay_up(item, cond):
        receive(item, cond)
        send(item, [(up, both(cond, has_up))] + to(x_devices, cond))

    def relay_down(item, cond):
        receive(item, cond)
        send(item, [(down, both(cond, has_down))] + to(x_devices, cond))

    def line(j):
        for piece in range(pieces):
            relay_up(ly((z - j) * nx + x, piece), z - j >= 1)
            relay_down(ly((z + j) * nx + x, piece), z + j <= nz - 1)

    if nz > 1:
        line(1)
    relay_up(lt(x), carries)
    relay_up(b(x, 0), carries)
    relay_up(ly(x, 0), z > 0)
    for j in range(2, nz):
        line(j)
        if j == 2:
            relay_up(ly(x, 1), z > 0)
    if nz <= 2:
        relay_up(ly(x, 1), z > 0)
    early = min(3, cols)
    for j in range(1, early):
        relay_up(b(x, j), carries)
    for other in y_others:
        item = (lxg.at[other * CORES + core], lx_base + other * CORES + core)
        receive(item, always)
        send(item, [(sibling, always)])
        from_owner = other * CORES + core < STEPS
        item = (slg.at[other * CORES + core], sl_base + other * CORES + core)
        receive(item, from_owner)
        send(item, [(sibling, from_owner)])
    for other in x_others:
        carried = other < STEPS if nx > STEPS else None
        receive(lt(other), carried)
        receive(b(other, 0), carried)
        for other_z in range(nz):
            receive(ly(other_z * nx + other, 0), always)
    for copy, cond in locals_:
        when(cond, copy.wait)
    send((ltop.at[pcol], ltg_base + pcol), to(y_devices + [sibling], always))
    send((stl.at[pcol], stl_base + pcol), to(y_devices + [sibling], owner_col), top.at[:, 0])
    send((rtop.at[pcol], rt_base + pcol), to(y_devices + [sibling], owner_col), lyg.at[:, 0])
    own = []
    for source, ref in ((top.at[:, 0], stl.at[pcol]), (lyg.at[:, 0], rtop.at[pcol])):
        copy = pltpu.make_async_copy(source, ref, local_sem.at[len(locals_) + len(own)])
        own.append(copy)
        when(owner_col, copy.start)
    for j in range(early, cols):
        relay_up(b(x, j), carries)
    for other in y_others:
        q = other * CORES + core
        item = (ltop.at[q], ltg_base + q)
        receive(item, always)
        send(item, [(sibling, always)])
        for ref, first in ((stl, stl_base), (rtop, rt_base)):
            item = (ref.at[q], first + q)
            receive(item, q < STEPS)
            send(item, [(sibling, q < STEPS)])
    for other_y in range(ny):
        q = other_y * CORES + (CORES - 1 - core)
        receive((lxg.at[q], lx_base + q), always)
        receive((ltop.at[q], ltg_base + q), always)
        for ref, first in ((slg, sl_base), (stl, stl_base), (rtop, rt_base)):
            receive((ref.at[q], first + q), q < STEPS)
    for other in x_others:
        carried = other < STEPS if nx > STEPS else None
        for other_z in range(nz):
            for piece in range(1, pieces):
                receive(ly(other_z * nx + other, piece), always)
        for j in range(1, cols):
            receive(b(other, j), carried)
    for copy in own:
        when(owner_col, copy.wait)
    for copy, cond in sends:
        when(cond, copy.wait_send)
    counts["send"] = len(sends)


def move(nx, st, lx, sl, ry):
    nprow, npcol = lax.axis_size("prow"), lax.axis_size("pcol")
    f32 = jnp.float32
    cols, size = st.shape[0], st.shape[1]
    shapes = [
        (STEPS,) + st.shape,
        (nprow,) + ry.shape,
        (npcol,) + lx.shape,
        (STEPS,) + sl.shape,
        (STEPS, STEPS, size, size),
        (STEPS, nprow) + ry.shape[1:],
        (npcol, STEPS) + lx.shape[1:],
    ]
    nz = nprow // nx
    receives = nprow * 2 + STEPS * cols + STEPS * 4 + npcol * 2
    fan = nx + npcol + 3
    sends = (cols + 4 + 2 * nz * 2 + cols + 8) * fan
    return pl.pallas_call(
        functools.partial(comm_kernel, nx, nprow, npcol, {}),
        out_shape=[jax.ShapeDtypeStruct(s, f32) for s in shapes],
        in_specs=[pl.BlockSpec(memory_space=pltpu.VMEM)] * 4,
        out_specs=[pl.BlockSpec(memory_space=pl.ANY)] * len(shapes),
        scratch_shapes=[
            pltpu.SemaphoreType.DMA((sends,)),
            pltpu.SemaphoreType.DMA((receives,)),
            pltpu.SemaphoreType.DMA((8,)),
        ],
        compiler_params=pltpu.CompilerParams(collective_id=0, has_side_effects=True),
    )(st, lx, sl, ry)


TILE = 128


def invert_kernel(in_ref, out_ref):
    count, order = in_ref.shape[0], in_ref.shape[1]
    tiles = order // TILE
    row = lax.broadcasted_iota(jnp.int32, (TILE, TILE), 0)
    col = lax.broadcasted_iota(jnp.int32, (TILE, TILE), 1)
    dot = functools.partial(jnp.dot, precision=HIGHEST, preferred_element_type=jnp.float32)
    out_ref[...] = jnp.zeros_like(out_ref)
    lows, invs = [], []
    for m in range(count):
        for t in range(tiles):
            low = in_ref[m, t * TILE : (t + 1) * TILE, t * TILE : (t + 1) * TILE]
            lows.append(low)
            invs.append(jnp.where(row == col, 1.0 / low, 0.0))
    span = 1
    while span < TILE:
        pick = jnp.logical_and(row // (2 * span) == col // (2 * span), jnp.logical_and(row // span % 2 == 1, col // span % 2 == 0))
        mids = [dot(jnp.where(pick, low, 0.0), inv) for low, inv in zip(lows, invs)]
        invs = [inv - dot(inv, mid) for mid, inv in zip(mids, invs)]
        span *= 2
    for m in range(count):
        for t in range(tiles):
            out_ref[m, t * TILE : (t + 1) * TILE, t * TILE : (t + 1) * TILE] = invs[m * tiles + t]
    span = TILE
    while span < order:
        for first in range(0, order, 2 * span):
            lo, mid, hi = first, first + span, first + 2 * span
            for m in range(count):
                inner = dot(in_ref[m, mid:hi, lo:mid], out_ref[m, lo:mid, lo:mid])
                out_ref[m, mid:hi, lo:mid] = -dot(out_ref[m, mid:hi, mid:hi], inner)
        span *= 2


def invert(lower):
    return pl.pallas_call(
        invert_kernel,
        out_shape=jax.ShapeDtypeStruct(lower.shape, lower.dtype),
        in_specs=[pl.BlockSpec(memory_space=pltpu.VMEM)],
        out_specs=pl.BlockSpec(memory_space=pltpu.VMEM),
    )(lower)


def shards(nx, cross_cov, left_factor, right_factor):
    nprow, npcol = lax.axis_size("prow"), lax.axis_size("pcol")
    prow, pcol = lax.axis_index("prow"), lax.axis_index("pcol")
    rows, _, size, cols, _, _ = cross_cov.shape
    depth = STEPS * size
    wide = depth // nprow
    fold = 128 // wide if wide < 128 else 1
    matrix = cross_cov.reshape(rows, size, cols, size)
    st = matrix[0].transpose(1, 0, 2)
    sl = matrix[:, :, 0]
    lx = left_factor[:, 0]
    ry = right_factor[:, 0].reshape(cols, fold, size // fold, wide).transpose(0, 2, 1, 3).reshape(cols, size // fold, fold * wide)
    top, lyg, lxg, slg, stl, rtop, ltop = move(nx, st, lx, sl, ry)

    def unfold(packed):
        groups = packed.shape[1]
        apart = packed.reshape(nprow, groups, size // fold, fold, wide)
        return apart.transpose(1, 3, 2, 0, 4).reshape(groups, size, depth)

    left_top = ltop.transpose(1, 2, 0, 3).reshape(depth, depth)
    right_top = unfold(rtop.transpose(1, 0, 2, 3)).reshape(depth, depth)
    left_inv, right_inv = invert(jnp.stack([left_top, right_top]))
    left = lxg.transpose(1, 2, 0, 3).reshape(rows, size, depth)
    right = unfold(lyg).reshape(cols, size, depth)

    def scaled(factor, inverse, index, axis_size):
        product = jnp.einsum("cij,jk->cik", factor, inverse, precision=HIGH)
        own = lax.dynamic_slice(inverse, (jnp.minimum(index, STEPS - 1) * size, 0), (size, depth))
        block = (jnp.arange(factor.shape[0]) * axis_size + index).reshape(-1, 1, 1)
        return jnp.where(block < STEPS, -own[None], product)

    w = scaled(left, left_inv, prow, nprow).reshape(rows * size, depth)
    v = scaled(right, right_inv, pcol, npcol).reshape(cols * size, depth)
    row_keep = (jnp.arange(rows) * nprow + prow >= STEPS).astype(jnp.float32)
    col_keep = (jnp.arange(cols) * npcol + pcol >= STEPS)
    corner = stl.transpose(1, 2, 0, 3).reshape(depth, depth)
    strip = slg.transpose(1, 2, 0, 3).reshape(rows, size, depth)
    strip = jnp.where(row_keep.reshape(-1, 1, 1) > 0, strip, 0.0).reshape(rows * size, depth)
    strip = strip - jnp.dot(w, corner, precision=HIGH)
    tops = jnp.where(col_keep.reshape(1, -1, 1, 1), top, 0.0).transpose(0, 2, 1, 3).reshape(depth, cols * size)
    a = jnp.concatenate([w, strip], 1)
    b = jnp.concatenate([tops, v.T], 0)
    update = jnp.dot(a, b, precision=HIGH).reshape(rows, size, cols, size)
    keep = (row_keep.reshape(-1, 1, 1, 1) > 0) & col_keep.reshape(1, 1, -1, 1)
    return (jnp.where(keep, matrix, 0.0) - update).reshape(cross_cov.shape)


def along_x(mesh):
    places = [getattr(d, "coords", None) for d in mesh.devices[:, 0]]
    if any(c is None for c in places):
        return STEPS
    return len({c[0] for c in places})


def solution(mesh):
    placed = (
        P(None, "prow", None, None, "pcol", None),
        P(None, "prow", None, "pcol"),
        P(None, "pcol", None, "prow"),
    )
    return jax.shard_map(
        functools.partial(shards, along_x(mesh)),
        mesh=mesh,
        in_specs=placed,
        out_specs=P(None, "prow", None, None, "pcol", None),
        check_vma=False,
    )
```

time: 611 us -> 273 us (0.45)
  waiting for transfers between devices: 392 us -> 0 us
  Pallas kernels: 0 us -> 140 us
  matrix products: 62.9 us -> 34 us
  other arithmetic: 48.3 us -> 20.8 us
  between operations: 14 us -> 0.37 us
  local copies, waits for them, and re-layouts: 85.6 us -> 73.8 us
    psum x4 -> x0, waiting for transfers between devices: 323 us -> none  [spread(): return lax.psum(jnp.where(mine, x, jnp.zeros_like(x)), axis)]
    pallas_call x0 -> x2, Pallas kernels: none -> 140 us  [the longest x1 128 us: move(): pl.pallas_call(functools.partial(comm_kernel, nx, nprow, npcol, {}), out_...]
    all_gather x2 -> x0, waiting for transfers between devices: 67.3 us -> none  [the longest x1 40.2 us: shards(): right_rows = lax.all_gather(right_factor, 'prow', axis=3, tiled=True)[:, 0]]
    another operation x9 -> x1, other arithmetic: 41.4 us -> 2.71 us  [shards(): left_inv, right_inv = invert(jnp.stack([left_top, right_top]))]
    dot_general x4, matrix products: 58 us -> 34 us  [the longest x1 17.7 us: shards(): update = jnp.dot(a, b, precision=HIGH).reshape(rows, size, cols, size)]
    reshape x1 -> x6, local copies, waits for them, and re-layouts: 12.7 us -> 32.4 us  [the longest x1 13.5 us: shards(): update = jnp.dot(a, b, precision=HIGH).reshape(rows, size, cols, size)]
    unnamed x7 -> x23, local copies, waits for them, and re-layouts: 32.7 us -> 14.9 us
    another operation x18 -> x5, local copies, waits for them, and re-layouts: 21.7 us -> 4.17 us  [the longest x4 2.76 us: shards(): left_inv, right_inv = invert(jnp.stack([left_top, right_top]))]
  transfers between devices with their start and end apart: 6 -> 0, of which waited for: 6 -> 0; matrix products, arithmetic and copies ran while one was open for 9% -> 0% of each run, Pallas kernels for 0% -> 0%
where the time goes in v1:
time: 273 us; the launch traced here: 269 us
  Pallas kernels  140 us (51%)
  local copies, waits for them, and re-layouts  73.8 us (27%)
  matrix products  34 us (12%)
  other arithmetic  20.8 us (8%)
    pallas_call x1, Pallas kernels, move(): pl.pallas_call(functools.partial(comm_kernel, nx, nprow, npcol, {}), out_...  128 us
    dot_general x1, matrix products, shards(): update = jnp.dot(a, b, precision=HIGH).reshape(rows, size, cols, size)  17.7 us
    unnamed x23, local copies, waits for them, and re-layouts  14.9 us
    sub x1, other arithmetic, shards(): return (jnp.where(keep, matrix, 0.0) - update).reshape(cross_cov.shape)  14.2 us
    reshape x1, local copies, waits for them, and re-layouts, shards(): update = jnp.dot(a, b, precision=HIGH).reshape(rows, size, cols, size)  13.5 us
    dot_general x2, matrix products, scaled(): product = jnp.einsum('cij,jk->cik', factor, inverse, precision=HIGH)  13 us
    pallas_call x1, Pallas kernels, invert(): pl.pallas_call(invert_kernel, out_shape=jax.ShapeDtypeStruct(lower.shape,...  11.7 us
    transpose x1, local copies, waits for them, and re-layouts, unfold(): return apart.transpose(1, 3, 2, 0, 4).reshape(groups, size, depth)  8.01 us

profile of v1, /device:TPU:0, one launch (start us, length us, event | category | flops | bytes accessed | tf_op | source)
XLA Modules:
  0.0 268.9 jit_solution(13139590201126061976)
XLA Ops:
  2.7 2.0 copy.62
  4.6 2.2 copy-done
  6.8 2.7 %copy.61 = f32[4,1,256,8,1,256]{5,2,0,3,4,1:T(8,128)S(1)} copy(f32[4,1,256,8,1,256]{5,4,3,2,1,0:T(1,128)S(1)} %copy-done) | data formatting | bytes 16777216 | tf_op args[0]
  10.5 128.3 %shard_map.37 = (f32[2,8,256,256]{3,2,1,0:T(8,128)}, f32[8,8,128,128]{3,2,1,0:T(8,128)}, f32[4,4,256,128]{3,2,1,0:T(8,128)}, f32[2,4,256,256]{3,2,1,0:T(8,128)},...) custom-call(f32[8,256,256]{2,1,0:T(8,128)} %bitcast.72, ...), custom_call_target="tpu_custom_call" | custom-call | tf_op jit(solution)/shard_map/pallas_call | solution.py:227
  138.9 2.0 copy.32
  143.8 2.7 %pad_maximum_fusion.in_ref = f32[2,512,512]{2,1,0:T(8,128)} fusion(f32[1,512,512]{2,1,0:T(8,128)S(1)} %reshape.145, f32[1,512,512]{2,1,0:T(8,128)} %stack_reshape.3), kind=kLoop, calls=%fused_computation.12 | loop fusion | flops 524288 | bytes 4194304 | tf_op jit(solution)/shard_map/stack | solution.py:306
  146.5 11.7 %shard_map.38 = f32[2,512,512]{2,1,0:T(8,128)} custom-call(f32[2,512,512]{2,1,0:T(8,128)} %pad_maximum_fusion.in_ref), custom_call_target="tpu_custom_call" | custom-call | tf_op jit(solution)/shard_map/pallas_call | solution.py:277
  159.1 1.8 copy.36
  161.0 3.0 %copy.51 = f32[4,256,2,256]{1,0,3,2:T(4,128)} copy(f32[4,256,2,256]{3,1,0,2:T(8,128)} %bitcast.80) | data formatting | bytes 4194304 | tf_op jit(solution)/shard_map/reshape | solution.py:321
  164.0 2.1 copy.56
  167.8 2.1 convolution_select_fusion.1
  171.3 3.3 %select_subtract_fusion = f32[1024,512]{0,1:T(8,128)} fusion(f32[1024,512]{0,1:T(8,128)S(1)} %bitcast.74, f32[1024,512]{1,0:T(8,128)S(1)} %bitcast.65, f32[512,512]{1,0:T(8,128)S(1)} %bitcast.79, pred[1024]{0:T(1024)(128)(4,1)S(1)} %broadcast_in_dim.84), kind=kOutput, calls=%fused_computation.14 | convolution fusion | flops 1611661312 | bytes 7341056 | tf_op jit(solution)/shard_map/dot_general | solution.py:323
  174.6 2.9 %copy.41 = f32[1024,512]{0,1:T(8,128)} copy(f32[1024,512]{1,0:T(8,128)} %bitcast.66) | data formatting | bytes 4194304 | tf_op jit(solution)/shard_map/reshape | solution.py:316
  177.5 2.8 %select_bitcast_fusion = f32[2,256,8,256]{3,1,2,0:T(8,128)S(1)} fusion(f32[2,8,256,256]{3,2,1,0:T(8,128)} %get-tuple-element.17, pred[8]{0:T(512)(128)(4,1)S(1)} %get-tuple-element.24), kind=kLoop, calls=%fused_computation.10 | loop fusion | flops 1048576 | bytes 8388616 | tf_op jit(solution)/shard_map/transpose | solution.py:324
  180.3 2.4 copy.42
  182.8 3.9 %copy.58 = f32[64,8,8,256]{3,1,2,0:T(8,128)} copy(f32[64,8,8,256]{3,2,1,0:T(8,128)S(1)} %bitcast.68) | data formatting | bytes 8388608
  186.7 5.7 %copy.43 = f32[8,8,128,128]{2,3,1,0:T(8,128)} copy(f32[8,8,128,128]{3,2,1,0:T(8,128)} %get-tuple-element.18) | data formatting | bytes 8388608 | tf_op jit(solution)/shard_map/pallas_call | solution.py:227
  192.4 8.0 %copy.44 = f32[8,2,128,8,64]{2,1,4,3,0:T(2,128)} copy(f32[8,2,128,8,64]{2,4,1,0,3:T(8,128)} %bitcast.69) | data formatting | bytes 8388608 | tf_op jit(solution)/shard_map/transpose | solution.py:302
  200.4 6.5 %reshape.148 = f32[8,256,512]{1,2,0:T(8,128)} reshape(f32[8,2,128,8,64]{2,1,4,3,0:T(2,128)} %copy.44) | data formatting | bytes 8388608 | tf_op jit(solution)/shard_map/reshape | solution.py:302
  206.9 10.9 %convolution_select_fusion = f32[8,256,512]{2,1,0:T(8,128)} fusion(f32[8,256,512]{1,2,0:T(8,128)} %reshape.148, f32[256,512]{1,0:T(8,128)S(1)} %copy-done.6, pred[8]{0:T(512)(128)(4,1)S(1)} %get-tuple-element.23, f32[2,512,512]{2,1,0:T(8,128)S(1)} %copy-done.1), kind=kOutput, calls=%fused_computation.11 | convolution fusion | flops 3222274048 | bytes 9961984 | tf_op jit(solution)/shard_map/cij,jk->cik/dot_general | solution.py:311
  217.8 5.5 %copy.46 = f32[2048,512]{0,1:T(8,128)} copy(f32[2048,512]{1,0:T(8,128)} %bitcast.67) | data formatting | bytes 8388608 | tf_op jit(solution)/shard_map/reshape | solution.py:317
  223.3 17.7 %fusion.1 = f32[1024,2048]{1,0:T(8,128)} fusion(f32[512,2048]{1,0:T(8,128)} %bitcast.77, f32[512,2048]{1,0:T(8,128)} %bitcast.76, f32[1024,512]{0,1:T(8,128)} %select_subtract_fusion, f32[1024,512]{0,1:T(8,128)S(1)} %copy-done.5), kind=kOutput, calls=%fused_computation.2 | convolution fusion | flops 12888047616 | bytes 20971520 | tf_op jit(solution)/shard_map/dot_general | solution.py:327
  241.0 13.5 %reshape.149 = f32[4,1,256,8,1,256]{5,4,3,2,1,0:T(1,128)} reshape(f32[1024,2048]{1,0:T(8,128)} %fusion.1) | data formatting | bytes 16777216 | tf_op jit(solution)/shard_map/reshape | solution.py:327
  254.5 14.2 %fusion = f32[4,1,256,8,1,256]{5,4,3,2,1,0:T(1,128)} fusion(f32[4,1,256,8,1,256]{5,4,3,2,1,0:T(1,128)} %reshape.149, f32[4,1,256,8,1,256]{5,4,3,2,1,0:T(1,128)} %param.3, pred[4,8]{1,0:T(4,128)(4,1)S(1)} %broadcast_and_fusion), kind=kLoop, calls=%fused_computation.1 | loop fusion | flops 4194304 | bytes 25165856 | tf_op jit(solution)/shard_map/sub | solution.py:329
  (36 shorter events, 10.6 us)
Async XLA Ops:
  0.0 2.7 slice-start
  2.7 4.1 %copy-start = (f32[4,1,256,8,1,256]{5,4,3,2,1,0:T(1,128)S(1)}, f32[4,1,256,8,1,256]{5,4,3,2,1,0:T(1,128)}, u32[]{:S(2)}) copy-start(f32[4,1,256,8,1,256]{5,4,3,2,1,0:T(1,128)} %param.3) | copy-start | bytes 25165828
  138.9 3.4 %copy-start.8 = (f32[2,8,128,128]{3,2,1,0:T(8,128)S(1)}, f32[2,8,128,128]{3,2,1,0:T(8,128)}, u32[]{:S(2)}) copy-start(f32[2,8,128,128]{3,2,1,0:T(8,128)} %get-tuple-element.13) | copy-start | bytes 3145732
  146.5 11.7 %copy-start.7 = (f32[2,2,256,256]{3,2,1,0:T(8,128)S(1)}, f32[2,2,256,256]{3,2,1,0:T(8,128)}, u32[]{:S(2)}) copy-start(f32[2,2,256,256]{3,2,1,0:T(8,128)} %get-tuple-element.16) | copy-start | bytes 3145732
  146.5 12.6 %copy-start.4 = (f32[4,4,256,128]{3,2,1,0:T(8,128)S(1)}, f32[4,4,256,128]{3,2,1,0:T(8,128)}, u32[]{:S(2)}) copy-start(f32[4,4,256,128]{3,2,1,0:T(8,128)} %get-tuple-element.14) | copy-start | bytes 6291460
  161.0 5.1 %copy-start.1 = (f32[2,512,512]{2,1,0:T(8,128)S(1)}, f32[2,512,512]{2,1,0:T(8,128)}, u32[]{:S(2)}) copy-start(f32[2,512,512]{2,1,0:T(8,128)} %shard_map.38) | copy-start | bytes 6291460
  166.1 1.8 copy-start.3
  170.0 1.3 copy-start.2
  200.4 6.5 %copy-start.6 = (f32[256,512]{1,0:T(8,128)S(1)}, f32[256,512]{1,0:T(8,128)}, u32[]{:S(2)}) copy-start(f32[256,512]{1,0:T(8,128)} %get-tuple-element.21) | copy-start | bytes 1572868
  217.8 5.5 %copy-start.5 = (f32[1024,512]{0,1:T(8,128)S(1)}, f32[1024,512]{0,1:T(8,128)}, u32[]{:S(2)}) copy-start(f32[1024,512]{0,1:T(8,128)} %copy.41) | copy-start | bytes 6291460

commit v2 on v1

--- a/solution.py
+++ b/solution.py
@@ -11,7 +11,6 @@
 CORES = 2
 MESH = pl.DeviceIdType.MESH
 HIGHEST = lax.Precision.HIGHEST
-HIGH = lax.Precision.HIGH
 
 
 def comm_kernel(nx, nprow, npcol, counts, st, lx, sl, ry, top, lyg, lxg, slg, stl, rtop, ltop, send_sem, recv_sem, local_sem):
@@ -111,7 +110,7 @@
             send((lxg.at[pcol], lx_base + pcol), to(y_devices + [sibling], always), lx)
             send((slg.at[pcol], sl_base + pcol), to(y_devices + [sibling], owner_col), sl)
     for j in range(1, cols):
-        send(b(x, j), [(up, lead)] + to(x_devices, lead), st.at[j])
+        send(b(x, j), [(up, lead)], st.at[j])
     locals_ = []
 
     def keep(source, ref, cond):
@@ -149,7 +148,9 @@
             relay_up(ly(x, 1), z > 0)
     if nz <= 2:
         relay_up(ly(x, 1), z > 0)
-    early = min(3, cols)
+    for j in range(1, cols):
+        send(b(x, j), to(x_devices, lead), st.at[j])
+    early = min(6, cols)
     for j in range(1, early):
         relay_up(b(x, j), carries)
     for other in y_others:
@@ -241,17 +242,32 @@
 TILE = 128
 
 
-def invert_kernel(in_ref, out_ref):
-    count, order = in_ref.shape[0], in_ref.shape[1]
+def halves(x):
+    high = x.astype(jnp.bfloat16)
+    return high, (x - high.astype(jnp.float32)).astype(jnp.bfloat16)
+
+
+def dot3(a, b, dims):
+    (ah, al), (bh, bl) = a, b
+    go = functools.partial(lax.dot_general, dimension_numbers=(dims, ((), ())), preferred_element_type=jnp.float32)
+    return go(ah, bh) + (go(ah, bl) + go(al, bh))
+
+
+NN = ((1,), (0,))
+NT = ((1,), (1,))
+
+
+def invert(low_ref, inv_ref):
+    count, order = low_ref.shape[0], low_ref.shape[1]
     tiles = order // TILE
     row = lax.broadcasted_iota(jnp.int32, (TILE, TILE), 0)
     col = lax.broadcasted_iota(jnp.int32, (TILE, TILE), 1)
     dot = functools.partial(jnp.dot, precision=HIGHEST, preferred_element_type=jnp.float32)
-    out_ref[...] = jnp.zeros_like(out_ref)
+    inv_ref[...] = jnp.zeros_like(inv_ref)
     lows, invs = [], []
     for m in range(count):
         for t in range(tiles):
-            low = in_ref[m, t * TILE : (t + 1) * TILE, t * TILE : (t + 1) * TILE]
+            low = low_ref[m, t * TILE : (t + 1) * TILE, t * TILE : (t + 1) * TILE]
             lows.append(low)
             invs.append(jnp.where(row == col, 1.0 / low, 0.0))
     span = 1
@@ -262,71 +278,115 @@
         span *= 2
     for m in range(count):
         for t in range(tiles):
-            out_ref[m, t * TILE : (t + 1) * TILE, t * TILE : (t + 1) * TILE] = invs[m * tiles + t]
+            inv_ref[m, t * TILE : (t + 1) * TILE, t * TILE : (t + 1) * TILE] = invs[m * tiles + t]
     span = TILE
     while span < order:
         for first in range(0, order, 2 * span):
             lo, mid, hi = first, first + span, first + 2 * span
             for m in range(count):
-                inner = dot(in_ref[m, mid:hi, lo:mid], out_ref[m, lo:mid, lo:mid])
-                out_ref[m, mid:hi, lo:mid] = -dot(out_ref[m, mid:hi, mid:hi], inner)
+                inner = dot(low_ref[m, mid:hi, lo:mid], inv_ref[m, lo:mid, lo:mid])
+                inv_ref[m, mid:hi, lo:mid] = -dot(inv_ref[m, mid:hi, mid:hi], inner)
         span *= 2
 
 
-def invert(lower):
+def unfolded(pieces, fold):
+    wide = pieces[0].shape[1] // fold
+    return jnp.concatenate(
+        [jnp.concatenate([piece[:, h * wide : (h + 1) * wide] for piece in pieces], 1) for h in range(fold)], 0
+    )
+
+
+def finish_kernel(nprow, npcol, fold, m_ref, top_ref, lyg_ref, lxg_ref, slg_ref, stl_ref, rtop_ref, ltop_ref, out_ref, low_ref, inv_ref, w_ref, s_ref, r_ref):
+    size = m_ref.shape[2]
+    total = m_ref.shape[1]
+    depth = STEPS * size
+    prow, pcol = lax.axis_index("prow"), lax.axis_index("pcol")
+    step = pl.program_id(0)
+
+    @pl.when(step == 0)
+    def _():
+        for k in range(STEPS):
+            span = slice(k * size, (k + 1) * size)
+            low_ref[0, span, :] = jnp.concatenate([ltop_ref[q, k] for q in range(npcol)], 1)
+            low_ref[1, span, :] = unfolded([rtop_ref[k, p] for p in range(nprow)], fold)
+        invert(low_ref, inv_ref)
+        left_inv = halves(inv_ref[0])
+        r_ref[0], r_ref[1] = halves(inv_ref[1])
+        left = jnp.concatenate([lxg_ref[q].reshape(total, depth // npcol) for q in range(npcol)], 1)
+        w = dot3(halves(left), left_inv, NN)
+        own = inv_ref[0, pl.ds(pl.multiple_of(jnp.minimum(prow, STEPS - 1) * size, size), size), :]
+        w_high, w_low = halves(w)
+        w_ref[0], w_ref[1] = w_high, w_low
+
+        @pl.when(prow < STEPS)
+        def _():
+            own_high, own_low = halves(-own)
+            w_ref[0, :size], w_ref[1, :size] = own_high, own_low
+
+        corner = jnp.concatenate([jnp.concatenate([stl_ref[k, b] for b in range(STEPS)], 0) for k in range(STEPS)], 1)
+        strip = jnp.concatenate([slg_ref[k].reshape(total, size) for k in range(STEPS)], 1)
+        row = lax.broadcasted_iota(jnp.int32, strip.shape, 0)
+        strip = jnp.where(jnp.logical_and(row < size, prow < STEPS), 0.0, strip)
+        strip = strip - dot3((w_ref[0], w_ref[1]), halves(corner), NN)
+        s_ref[0], s_ref[1] = halves(strip)
+
+    solved_col = jnp.logical_and(step == 0, pcol < STEPS)
+    right = unfolded([lyg_ref[p, 0] for p in range(nprow)], fold)
+    v = dot3(halves(right), (r_ref[0], r_ref[1]), NN)
+    own = inv_ref[1, pl.ds(pl.multiple_of(jnp.minimum(pcol, STEPS - 1) * size, size), size), :]
+    v = jnp.where(solved_col, -own, v)
+    tops = jnp.concatenate([top_ref[k, 0] for k in range(STEPS)], 0)
+    tops = jnp.where(solved_col, 0.0, tops)
+    update = dot3((w_ref[0], w_ref[1]), halves(tops), NN) + dot3((s_ref[0], s_ref[1]), halves(v), NT)
+    row = lax.broadcasted_iota(jnp.int32, (total, size), 0)
+    gone = jnp.logical_or(solved_col, jnp.logical_and(row < size, prow < STEPS))
+    out_ref[0] = jnp.where(gone, 0.0, m_ref[0]) - update
+
+
+def finish(fold, m, top, lyg, lxg, slg, stl, rtop, ltop):
+    nprow, npcol = lax.axis_size("prow"), lax.axis_size("pcol")
+    cols, total, size = m.shape
+    depth = STEPS * size
+
+    def whole(x):
+        return pl.BlockSpec(x.shape, lambda d: (0,) * x.ndim)
+
+    block = pl.BlockSpec((1, total, size), lambda d: (d, 0, 0))
     return pl.pallas_call(
-        invert_kernel,
-        out_shape=jax.ShapeDtypeStruct(lower.shape, lower.dtype),
-        in_specs=[pl.BlockSpec(memory_space=pltpu.VMEM)],
-        out_specs=pl.BlockSpec(memory_space=pltpu.VMEM),
-    )(lower)
+        functools.partial(finish_kernel, nprow, npcol, fold),
+        grid=(cols,),
+        out_shape=jax.ShapeDtypeStruct(m.shape, m.dtype),
+        in_specs=[
+            block,
+            pl.BlockSpec((STEPS, 1, size, size), lambda d: (0, d, 0, 0)),
+            pl.BlockSpec((nprow, 1) + lyg.shape[2:], lambda d: (0, d, 0, 0)),
+        ]
+        + [whole(x) for x in (lxg, slg, stl, rtop, ltop)],
+        out_specs=block,
+        scratch_shapes=[
+            pltpu.VMEM((2, depth, depth), jnp.float32),
+            pltpu.VMEM((2, depth, depth), jnp.float32),
+            pltpu.VMEM((2, total, depth), jnp.bfloat16),
+            pltpu.VMEM((2, total, depth), jnp.bfloat16),
+            pltpu.VMEM((2, depth, depth), jnp.bfloat16),
+        ],
+        compiler_params=pltpu.CompilerParams(dimension_semantics=("arbitrary",), vmem_limit_bytes=56 * 1024 * 1024),
+    )(m, top, lyg, lxg, slg, stl, rtop, ltop)
 
 
 def shards(nx, cross_cov, left_factor, right_factor):
-    nprow, npcol = lax.axis_size("prow"), lax.axis_size("pcol")
-    prow, pcol = lax.axis_index("prow"), lax.axis_index("pcol")
+    nprow = lax.axis_size("prow")
     rows, _, size, cols, _, _ = cross_cov.shape
-    depth = STEPS * size
-    wide = depth // nprow
-    fold = 128 // wide if wide < 128 else 1
-    matrix = cross_cov.reshape(rows, size, cols, size)
-    st = matrix[0].transpose(1, 0, 2)
-    sl = matrix[:, :, 0]
+    wide = STEPS * size // nprow
+    fold = TILE // wide if wide < TILE else 1
+    m = cross_cov.transpose(3, 0, 1, 2, 4, 5).reshape(cols, rows * size, size)
+    st = m[:, :size]
+    sl = m[0].reshape(rows, size, size)
     lx = left_factor[:, 0]
     ry = right_factor[:, 0].reshape(cols, fold, size // fold, wide).transpose(0, 2, 1, 3).reshape(cols, size // fold, fold * wide)
-    top, lyg, lxg, slg, stl, rtop, ltop = move(nx, st, lx, sl, ry)
-
-    def unfold(packed):
-        groups = packed.shape[1]
-        apart = packed.reshape(nprow, groups, size // fold, fold, wide)
-        return apart.transpose(1, 3, 2, 0, 4).reshape(groups, size, depth)
-
-    left_top = ltop.transpose(1, 2, 0, 3).reshape(depth, depth)
-    right_top = unfold(rtop.transpose(1, 0, 2, 3)).reshape(depth, depth)
-    left_inv, right_inv = invert(jnp.stack([left_top, right_top]))
-    left = lxg.transpose(1, 2, 0, 3).reshape(rows, size, depth)
-    right = unfold(lyg).reshape(cols, size, depth)
-
-    def scaled(factor, inverse, index, axis_size):
-        product = jnp.einsum("cij,jk->cik", factor, inverse, precision=HIGH)
-        own = lax.dynamic_slice(inverse, (jnp.minimum(index, STEPS - 1) * size, 0), (size, depth))
-        block = (jnp.arange(factor.shape[0]) * axis_size + index).reshape(-1, 1, 1)
-        return jnp.where(block < STEPS, -own[None], product)
-
-    w = scaled(left, left_inv, prow, nprow).reshape(rows * size, depth)
-    v = scaled(right, right_inv, pcol, npcol).reshape(cols * size, depth)
-    row_keep = (jnp.arange(rows) * nprow + prow >= STEPS).astype(jnp.float32)
-    col_keep = (jnp.arange(cols) * npcol + pcol >= STEPS)
-    corner = stl.transpose(1, 2, 0, 3).reshape(depth, depth)
-    strip = slg.transpose(1, 2, 0, 3).reshape(rows, size, depth)
-    strip = jnp.where(row_keep.reshape(-1, 1, 1) > 0, strip, 0.0).reshape(rows * size, depth)
-    strip = strip - jnp.dot(w, corner, precision=HIGH)
-    tops = jnp.where(col_keep.reshape(1, -1, 1, 1), top, 0.0).transpose(0, 2, 1, 3).reshape(depth, cols * size)
-    a = jnp.concatenate([w, strip], 1)
-    b = jnp.concatenate([tops, v.T], 0)
-    update = jnp.dot(a, b, precision=HIGH).reshape(rows, size, cols, size)
-    keep = (row_keep.reshape(-1, 1, 1, 1) > 0) & col_keep.reshape(1, 1, -1, 1)
-    return (jnp.where(keep, matrix, 0.0) - update).reshape(cross_cov.shape)
+    moved = move(nx, st, lx, sl, ry)
+    out = finish(fold, m, *moved)
+    return out.reshape(cols, rows, 1, size, 1, size).transpose(1, 2, 3, 0, 4, 5)
 
 
 def along_x(mesh):

time: 273 us -> 179 us (0.66)
  the two profiles are of different devices: /device:TPU:0 before, /device:TPU:24 now
where the time goes in v2:
time: 179 us
  Pallas kernels  154 us (86%)
  local copies, waits for them, and re-layouts  24.6 us (14%)
    pallas_call x1, Pallas kernels, move(): pl.pallas_call(functools.partial(comm_kernel, nx, nprow, npcol, {}), out_...  118 us
    pallas_call x1, Pallas kernels, finish(): pl.pallas_call(functools.partial(finish_kernel, nprow, npcol, fold), grid...  36.3 us
    reshape x1, local copies, waits for them, and re-layouts, shards(): return out.reshape(cols, rows, 1, size, 1, size).transpose(1, 2, 3, 0, 4, 5)  11 us
    unnamed x3, local copies, waits for them, and re-layouts  8.64 us

profile of v2, /device:TPU:24, one launch (start us, length us, event | category | flops | bytes accessed | tf_op | source)
XLA Modules:
  0.0 178.5 jit_solution(4602234480008600219)
XLA Ops:
  0.0 1.3 reshape_squeeze.7
  1.4 1.0 copy.12.ry
  2.4 6.1 %copy.18 = f32[4,1,256,8,1,256]{5,2,0,4,1,3:T(8,128)S(1)} copy(f32[4,1,256,8,1,256]{5,4,3,2,1,0:T(1,128)} %param.3) | data formatting | bytes 16777216 | tf_op args[0]
  8.4 0.0 copy-start
  8.4 1.1 slice_bitcast_fusion.sl
  9.6 2.6 %copy-done = f32[4,1,256,8,1,256]{5,2,0,4,1,3:T(8,128)} copy-done((f32[4,1,256,8,1,256]{5,2,0,4,1,3:T(8,128)}, f32[4,1,256,8,1,256]{5,2,0,4,1,3:T(8,128)S(1)}, u32[]{:S(2)}) %copy-start) | copy-done | bytes 8388632
  12.1 1.5 slice.9.st
  13.6 117.5 %shard_map.37 = (f32[2,8,256,256]{3,2,1,0:T(8,128)}, f32[8,8,128,128]{3,2,1,0:T(8,128)}, f32[4,4,256,128]{3,2,1,0:T(8,128)}, f32[2,4,256,256]{3,2,1,0:T(8,128)},...) custom-call(f32[8,256,256]{2,1,0:T(8,128)} %slice.9.st, ...), custom_call_target="tpu_custom_call" | custom-call | tf_op jit(solution)/shard_map/pallas_call | solution.py:228
  131.1 36.3 %shard_map.38 = f32[8,1024,256]{2,1,0:T(8,128)} custom-call(f32[8,1024,256]{2,1,0:T(8,128)} %bitcast.20, f32[2,8,256,256]{3,2,1,0:T(8,128)} %get-tuple-element.12.top_ref, f32[8,8,128,128]{3,2,1,0:T(8,128)} %get-tuple-element.13.lyg_ref, f32[4,4,256,128]{3,2,1,0:T(8,128)} %get-tuple-element.14.lxg_ref, f32[2,4,256,256]{3,2,1,0:T(8,128)} %get-tuple-element.15.slg_ref, ...), custom_call_target="tpu_custom_call" | custom-call | tf_op jit(solution)/shard_map/pallas_call | solution.py:355
  167.5 11.0 %copy.17 = f32[8,4,1,256,1,256]{5,4,0,3,2,1:T(1,128)} copy(f32[8,4,1,256,1,256]{5,3,1,0,4,2:T(8,128)} %bitcast.21) | data formatting | bytes 16777216 | tf_op jit(solution)/shard_map/reshape | solution.py:389
  (1 shorter events, 0.0 us)
Async XLA Ops:
  8.4 3.7 %copy-start = (f32[4,1,256,8,1,256]{5,2,0,4,1,3:T(8,128)}, f32[4,1,256,8,1,256]{5,2,0,4,1,3:T(8,128)S(1)}, u32[]{:S(2)}) copy-start(f32[4,1,256,8,1,256]{5,2,0,4,1,3:T(8,128)S(1)} %copy.18) | copy-start | bytes 25165828
